TPU v7x, 512 devices: a 4x2x32 block of a 4x16x32 slice. The times are simulated.
512 devices in a mesh: groups: 2 (over y), seq: 32 (over z), head: 8 (over x, core).
Axes of the slice: x: 4, y: 2, z: 32, core: 2. Of those that a mesh axis runs over, the one named last changes fastest.
The devices are a block of a 4x16x32 slice.
Arguments:
- residual: bfloat16 [8192, 2048], P(('groups', 'seq')), parts along dimension 0, may hold values from -6 to 6
- query_in: bfloat16 [8192, 2048], P(('groups', 'seq'), 'head'), parts along dimension 0, may hold values from -6 to 6
- key_in: bfloat16 [8192, 2048], P(('groups', 'seq'), 'head'), parts along dimension 0, may hold values from -6 to 6
- value_in: bfloat16 [8192, 4096], P(('groups', 'seq'), 'head'), parts along dimension 0, may hold values from -6 to 6
- gating_in: bfloat16 [8192, 4096], P(('groups', 'seq'), 'head'), parts along dimension 0, may hold values from -6 to 6
- beta_logit: float32 [8192, 32], P(('groups', 'seq'), 'head'), parts along dimension 0, may hold values from -12 to 2
- decay_logit: float32 [8192, 32], P(('groups', 'seq'), 'head'), parts along dimension 0, may hold values from -16 to 1
- seq_length: int32 [2], P('groups'), parts along dimension 0, may hold values from 2048 to 4096
- conv_query: float32 [4, 2048], P(None, 'head'), may hold values from -3 to 3
- conv_key: float32 [4, 2048], P(None, 'head'), may hold values from -3 to 3
- conv_value: float32 [4, 4096], P(None, 'head'), may hold values from -3 to 3
- decay_rate: float32 [32], P('head'), may hold values from 0.5 to 136
- norm_gain: float32 [128], replicated, may hold values from 0.1 to 1.9
- out_weight: bfloat16 [4096, 2048], P('head'), may hold values from -0.09375 to 0.09375
- attn_gain: float32 [2048], replicated, may hold values from 0.1 to 1.9
- query_weight: bfloat16 [2048, 8192], P('seq', 'head'), may hold values from -1 to 1
- key_value_weight: bfloat16 [2048, 1024], P('seq'), may hold values from -10 to 10
Outputs:
- hidden_out: bfloat16 [8192, 2048], P(('groups', 'seq')), parts along dimension 0
- attention_out: bfloat16 [8192, 4096], P(('groups', 'seq'), 'head'), parts along dimension 0
There are 2 independent parts, one for each index of `groups`. A program takes and returns all parts, laid end to end along the dimension named above; an argument that names none is the same for every part. Nothing has to cross between parts.
All inputs are finite; a program needn't handle non-finite values.
Results may differ from a plain program's by a relative error of at most 0.02.
The roundings to bfloat16 on the way count: a program that leaves them out, or rounds other values in their place, can miss the bound.
Values may be sent and summed in bfloat16 or wider, within the bound.
A program may use at most 128 MiB of HBM per device.

v0:
```python
import jax
import jax.numpy as jnp
from jax import lax
from jax.sharding import PartitionSpec as P

DK = 128
DV = 128
QUERY_HEADS = 16
KEY_VALUE_HEADS = 2
HEAD_WIDTH = 256
CONV = 4
SPAN = 64


EPSILON = 1e-06
NEGATIVE = -1e30


def shifted(shard, axis, by):
    count = lax.axis_size(axis)
    pairs = [(i, i + by) for i in range(count) if 0 <= i + by < count]
    return lax.ppermute(shard, axis, pairs)


def entering_2(shard, axis, combine, identity):
    count, mine = (lax.axis_size(axis), lax.axis_index(axis))
    everything = jax.tree.map(lambda part: lax.all_gather(part, axis), shard)
    start = jax.tree.map(
        lambda part, zero: jnp.broadcast_to(jnp.asarray(zero, part.dtype), part.shape),
        shard,
        identity,
    )

    def hop(k, before):
        reached = k < mine
        new = combine(before, jax.tree.map(lambda part: part[k], everything))
        return jax.tree.map(lambda a, b: jnp.where(reached, a, b), new, before)

    return lax.fori_loop(0, count, hop, start)


def split_up(shard, dim, count):
    before, after = (shard.shape[:dim], shard.shape[dim + 1 :])
    return jnp.moveaxis(shard.reshape(*before, count, -1, *after), dim, 0)


def sum_at_owner(shard, axis, dim):
    count = lax.axis_size(axis)
    tiles = lax.all_to_all(split_up(shard, dim, count), axis, 0, 0, tiled=True)
    return jnp.sum(tiles, axis=0)


def in_one_piece(arrays, axis, dim, along):
    ends, at = ([], 0)
    for a in arrays[:-1]:
        at += a.shape[along]
        ends.append(at)
    both = jnp.concatenate(arrays, axis=along)
    return tuple(jnp.split(lax.all_gather(both, axis, axis=dim, tiled=True), ends, axis=along))


def conv_silu(inputs, tail_rows, kernel):
    joined = jnp.concatenate([tail_rows, inputs], 0).astype(jnp.float32)
    row_total = inputs.shape[0]
    summed = jnp.zeros((row_total, inputs.shape[1]), jnp.float32)
    for offset in range(CONV):
        summed = summed + kernel[offset] * joined[offset : offset + row_total]
    return jax.nn.silu(summed)


def unit_rows(tensor):
    return tensor / jnp.sqrt(jnp.sum(tensor * tensor, -1, keepdims=True) + EPSILON)


def rms_scaled(tensor, gain_vector):
    return tensor * lax.rsqrt(jnp.mean(tensor * tensor, -1, keepdims=True) + EPSILON) * gain_vector


def span_terms(queries, keyset, values, betas, log_decay):
    highest_index = lax.Precision.HIGHEST
    running_totals = jnp.cumsum(log_decay, -1)
    block_size = log_decay.shape[-1]
    order_ids = jnp.arange(block_size)
    inclusive = order_ids[:, None] >= order_ids[None, :]
    strict = order_ids[:, None] > order_ids[None, :]
    spread = running_totals[..., :, None] - running_totals[..., None, :]
    within = jnp.where(inclusive, jnp.exp(jnp.where(inclusive, spread, 0.0)), 0.0)
    key_gram = jnp.einsum("nhik,nhjk->nhij", keyset, keyset, precision=highest_index)
    lower_part = jnp.where(strict, betas[..., :, None] * within * key_gram, 0.0) + jnp.eye(
        block_size, dtype=jnp.float32
    )
    right_side = jnp.concatenate(
        [(betas * jnp.exp(running_totals))[..., None] * keyset, betas[..., None] * values], -1
    )
    solved = jax.scipy.linalg.solve_triangular(
        lower_part, right_side, lower=True, unit_diagonal=True
    )
    key_width = keyset.shape[-1]
    weights_w = solved[..., :key_width]
    updates = solved[..., key_width:]
    mixing = jnp.einsum("nhik,nhjk->nhij", queries, keyset, precision=highest_index) * within
    local_out = jnp.einsum("nhij,nhjv->nhiv", mixing, updates, precision=highest_index)
    carry_map = jnp.exp(running_totals)[..., None] * queries - jnp.einsum(
        "nhij,nhjk->nhik", mixing, weights_w, precision=highest_index
    )
    stop_boundary = jnp.exp(running_totals[..., -1:] - running_totals)[..., None] * keyset
    transition = jnp.exp(running_totals[..., -1])[..., None, None] * jnp.eye(
        key_width, dtype=jnp.float32
    ) - jnp.einsum("nhjk,nhjl->nhkl", stop_boundary, weights_w, precision=highest_index)
    injected = jnp.einsum("nhjk,nhjv->nhkv", stop_boundary, updates, precision=highest_index)
    return (local_out, carry_map, transition, injected)


def compose_pair(earlier_rows, later_rows):
    highest_index = lax.Precision.HIGHEST
    return (
        jnp.einsum("hkl,hlm->hkm", later_rows[0], earlier_rows[0], precision=highest_index),
        jnp.einsum("auf,afi->aui", later_rows[0], earlier_rows[1], precision=highest_index)
        + later_rows[1],
    )


def shards(
    residual,
    query_in,
    key_in,
    value_in,
    gating_in,
    beta_logit,
    decay_logit,
    seq_length,
    conv_query,
    conv_key,
    conv_value,
    decay_rate,
    norm_gain,
    out_weight,
    attn_gain,
    query_weight,
    key_value_weight,
):
    highest_index = lax.Precision.HIGHEST
    row_count = residual.shape[0]
    seq_rank = lax.axis_index("seq")
    positions = seq_rank * row_count + jnp.arange(row_count, dtype=jnp.int32)
    length_now = seq_length[0]
    alive_mask = (positions < length_now).astype(jnp.float32)
    rim_start = row_count - CONV + 1
    tails = shifted((query_in[rim_start:], key_in[rim_start:], value_in[rim_start:]), "seq", 1)
    key_heads = query_in.shape[1] // DK
    value_heads = value_in.shape[1] // DV
    queries = unit_rows(
        conv_silu(query_in, tails[0], conv_query).reshape(row_count, key_heads, DK)
    ) * DK ** (-0.5)
    keyset = unit_rows(conv_silu(key_in, tails[1], conv_key).reshape(row_count, key_heads, DK))
    values = conv_silu(value_in, tails[2], conv_value).reshape(row_count, value_heads, DV)
    queries = jnp.repeat(queries, value_heads // key_heads, axis=1)
    keyset = jnp.repeat(keyset, value_heads // key_heads, axis=1)
    betas = jax.nn.sigmoid(beta_logit) * alive_mask[:, None]
    log_decay = -decay_rate[None, :] * jax.nn.softplus(decay_logit) * alive_mask[:, None]
    span_count = row_count // SPAN

    def to_spans(tensor):
        return tensor.reshape(span_count, SPAN, value_heads, tensor.shape[2]).transpose(0, 2, 1, 3)

    local_out, carry_map, transition, injected = span_terms(
        to_spans(queries),
        to_spans(keyset),
        to_spans(values),
        betas.reshape(span_count, SPAN, value_heads).transpose(0, 2, 1),
        log_decay.reshape(span_count, SPAN, value_heads).transpose(0, 2, 1),
    )
    identity_map = jnp.broadcast_to(jnp.eye(DK, dtype=jnp.float32), (value_heads, DK, DK))
    empty_state = jnp.zeros((value_heads, DK, DV), jnp.float32)

    def compose_spans(running, pair_now):
        return (compose_pair(running, pair_now), running)

    device_pair, prefix_pair = lax.scan(
        compose_spans, (identity_map, empty_state), (transition, injected)
    )
    entering = entering_2(device_pair, "seq", compose_pair, (identity_map, empty_state))[1]
    span_states = (
        jnp.einsum("nhkl,hlv->nhkv", prefix_pair[0], entering, precision=highest_index)
        + prefix_pair[1]
    )
    outputs = local_out + jnp.einsum(
        "nhik,nhkv->nhiv", carry_map, span_states, precision=highest_index
    )
    outputs = outputs.transpose(0, 2, 1, 3).reshape(row_count, value_heads, DV)
    gating = gating_in.astype(jnp.float32).reshape(row_count, value_heads, DV)
    gated = (
        (rms_scaled(outputs, norm_gain) * jax.nn.silu(gating))
        .astype(jnp.bfloat16)
        .reshape(row_count, value_heads * DV)
    )
    share_rows = row_count // lax.axis_size("head")
    first_row = lax.axis_index("head") * share_rows
    summed = sum_at_owner(jnp.dot(gated, out_weight, preferred_element_type=jnp.float32), "head", 0)
    own_rows = lax.dynamic_slice_in_dim(residual, first_row, share_rows, 0)
    hidden_part = (own_rows.astype(jnp.float32) + summed).astype(jnp.bfloat16)
    normed_part = rms_scaled(hidden_part.astype(jnp.float32), attn_gain).astype(jnp.bfloat16)
    hidden_out, normalized = (
        lax.all_gather(hidden_part, "head", axis=0, tiled=True),
        lax.all_gather(normed_part, "head", axis=0, tiled=True),
    )
    attention_channel_id = lax.axis_index("head")
    query_head_rows = query_weight.shape[1] // (2 * HEAD_WIDTH)
    key_value_head = attention_channel_id * query_head_rows // (QUERY_HEADS // KEY_VALUE_HEADS)
    key_start = key_value_head * HEAD_WIDTH
    value_offset = (KEY_VALUE_HEADS + key_value_head) * HEAD_WIDTH
    picked = jnp.concatenate(
        [
            lax.dynamic_slice_in_dim(key_value_weight, key_start, HEAD_WIDTH, 1),
            lax.dynamic_slice_in_dim(key_value_weight, value_offset, HEAD_WIDTH, 1),
        ],
        1,
    )
    pieces = in_one_piece((query_weight, picked), "seq", 0, 1)
    query_proj = jnp.dot(normalized, pieces[0], preferred_element_type=jnp.float32)
    kv_proj = jnp.dot(normalized, pieces[1], preferred_element_type=jnp.float32)
    key_rows = kv_proj[:, :HEAD_WIDTH].astype(jnp.bfloat16)
    value_rows = kv_proj[:, HEAD_WIDTH:].astype(jnp.bfloat16)
    query_proj = query_proj.reshape(row_count, query_head_rows, 2, HEAD_WIDTH)
    queries_att = query_proj[:, :, 0].astype(jnp.bfloat16)
    gating_att = query_proj[:, :, 1]
    half_rows = row_count // 2
    blocks = (queries_att[:half_rows], queries_att[half_rows:])
    block_positions = (positions[:half_rows], positions[half_rows:])
    start_state = (
        jnp.full((query_head_rows, half_rows), NEGATIVE, jnp.float32),
        jnp.zeros((query_head_rows, half_rows), jnp.float32),
        jnp.zeros((query_head_rows, half_rows, HEAD_WIDTH), jnp.float32),
    )
    running = (start_state, start_state)
    offset = jnp.int32(0)
    key_piece, value_piece = in_one_piece((key_rows, value_rows), "seq", 0, 1)
    key_positions = jnp.arange(key_piece.shape[0], dtype=jnp.int32)
    updated = []
    for block_index in range(2):
        block_queries = blocks[block_index]
        query_positions = block_positions[block_index]
        needed = jnp.logical_and(offset <= query_positions[-1], offset < length_now)

        def refresh(recurrent_state):
            peak, total, accum = recurrent_state
            scores = jnp.einsum(
                "qhd,kd->hqk", block_queries, key_piece, preferred_element_type=jnp.float32
            ) * HEAD_WIDTH ** (-0.5)
            visible = (key_positions[None, :] <= query_positions[:, None]) & (
                key_positions[None, :] < length_now
            )
            scores = jnp.where(visible[None], scores, NEGATIVE)
            new_peak = jnp.maximum(peak, jnp.max(scores, -1))
            weights = jnp.where(visible[None], jnp.exp(scores - new_peak[..., None]), 0.0)
            return (
                new_peak,
                jnp.sum(weights, -1),
                jnp.einsum(
                    "hqk,kd->hqd",
                    weights.astype(jnp.bfloat16),
                    value_piece,
                    preferred_element_type=jnp.float32,
                ),
            )

        updated.append(
            lax.cond(needed, refresh, lambda recurrent_state: recurrent_state, running[block_index])
        )
    finished = tuple(updated)
    results = [
        (recurrent_state[2] / recurrent_state[1][..., None]).transpose(1, 0, 2)
        for recurrent_state in finished
    ]
    attended = jnp.concatenate(results, 0)
    attention_out = (
        (attended * jax.nn.sigmoid(gating_att))
        .astype(jnp.bfloat16)
        .reshape(row_count, query_head_rows * HEAD_WIDTH)
    )
    return (hidden_out, attention_out)


def solution(mesh):
    placed = (
        P(("groups", "seq"), None),
        P(("groups", "seq"), "head"),
        P(("groups", "seq"), "head"),
        P(("groups", "seq"), "head"),
        P(("groups", "seq"), "head"),
        P(("groups", "seq"), "head"),
        P(("groups", "seq"), "head"),
        P("groups"),
        P(None, "head"),
        P(None, "head"),
        P(None, "head"),
        P("head"),
        P(),
        P("head", None),
        P(),
        P("seq", "head"),
        P("seq", None),
    )
    return jax.shard_map(
        shards,
        mesh=mesh,
        in_specs=placed,
        out_specs=(P(("groups", "seq"), None), P(("groups", "seq"), "head")),
        check_vma=False,
    )
```

profile of v0, /device:TPU:38, one launch (start us, length us, event | category | flops | bytes accessed | tf_op | source)
XLA Modules:
  0.0 695.1 jit_solution(13250883313684611276)
XLA Ops:
  8.1 4.7 collective-permute-start.1
  13.5 4.7 collective-permute-start.2
  25.2 39.3 %custom-call.4 = f32[2,4,1,64,64]{3,4,2,1,0:T(8,128)S(1)} custom-call(f32[2,4,1,64,64]{4,3,2,1,0:T(8,128)S(1)} %fusion.57), custom_call_target="InvertDiagBlocksLowerTriangular" | custom-call | tf_op jit(solution)/shard_map/jit(_solve_triangular)/vmap(vmap())/triangular_solve | solution.py:95
  65.8 1.9 fusion.83
  68.9 8.3 %while.31 = (s32[]{:T(128)}, f32[4,128,128]{2,1,0:T(8,128)S(1)}, f32[4,128,128]{2,1,0:T(8,128)S(1)}, f32[2,4,128,128]{3,2,1,0:T(8,128)}, f32[2,4,128,128]{2,3,1,...) while((s32[]{:T(128)}, f32[4,128,128]{2,1,0:T(8,128)S(1)}, ...), condition=%wide.region_4.5_spmd.clone, body=%wide.region_3.4_spmd.clone.sunk | while | flops 201523200 | bytes 6031496 | solution.py:179
  68.9 2.0 convolution_add_fusion.4
  73.1 2.0 convolution_add_fusion.4
  79.6 4.9 collective-permute-start
  91.1 160.1 %all-gather.11.cloned.1.call-done = f32[128,128,128]{2,1,0:T(8,128)} async-done(((f32[4,128,128]{2,1,0:T(8,128)}), f32[128,128,128]{2,1,0:T(8,128)}) %all-gather.11.cloned.1.call-update) | async-done | bytes 8388624 | tf_op jit(solution)/shard_map/all_gather | solution.py:27
  251.1 143.9 %all-gather.13.cloned.1.call-done = f32[128,128,128]{2,1,0:T(8,128)} async-done(((f32[4,128,128]{2,1,0:T(8,128)}), f32[128,128,128]{2,1,0:T(8,128)}) %all-gather.13.cloned.1.call-update) | async-done | bytes 8388624 | tf_op jit(solution)/shard_map/all_gather | solution.py:27
  395.0 47.5 %while.32 = (s32[]{:T(128)}, f32[4,128,128]{2,1,0:T(8,128)S(1)}, s32[]{:T(128)}, f32[32,4,128,128]{3,2,1,0:T(8,128)}, f32[32,4,128,128]{3,2,1,0:T(8,128)}, /*index=5*/s32[]{:T(128)}, s32[]{:T(128)}) while((s32[]{:T(128)}, f32[4,128,128]{2,1,0:T(8,128)S(1)}, s32[]{:T(128)}, f32[32,4,128,128]{3,2,1,0:T(8,128)}, ...), condition=%wide.region_6.7_spmd.clone, body=%wide.region_5.6_spmd.clone.sunk | while | flops 100925440 | bytes 1837663 | solution.py:39
  420.2 1.4 fusion.142
  427.7 1.4 fusion.142
  430.6 1.4 fusion.142
  435.1 1.4 fusion.142
  442.5 1.9 fusion.51
  446.2 1.4 fusion.49
  447.7 4.9 all-to-all-start
  452.6 13.9 %all-to-all-done = f32[8,16,2048]{2,1,0:T(8,128)S(1)} async-done(((f32[8,16,2048]{2,1,0:T(8,128)}), f32[8,16,2048]{2,1,0:T(8,128)S(1)}, u32[]{:S(2)}, u32[]{:S(2)}) %all-to-all-start) | async-done | bytes 1048608 | tf_op jit(solution)/shard_map/all_to_all | solution.py:49
  467.6 13.2 %all_gather.29 = bf16[128,2048]{1,0:T(8,128)(2,1)S(1)} all-gather(bf16[16,2048]{1,0:T(8,128)(2,1)S(1)} %fusion.93), channel_id=1, replica_groups=mesh['groups'=2,'seq'=32,'head'=8] {'head'}, dimensions={0}, use_global_device_ids=true | all-gather | bytes 589824 | tf_op jit(solution)/shard_map/all_gather | solution.py:205
  480.8 53.3 %all-gather.7.cloned.1.call-done = bf16[2048,1536]{1,0:T(8,128)(2,1)} async-done(((bf16[64,1536]{1,0:T(8,128)(2,1)}), bf16[2048,1536]{1,0:T(8,128)(2,1)}) %all-gather.7.cloned.1.call-update) | async-done | bytes 6291472 | tf_op jit(solution)/shard_map/all_gather | solution.py:59
  534.1 2.7 fusion.58
  538.8 3.9 fusion.45
  543.2 13.2 %all_gather.28 = bf16[128,2048]{1,0:T(8,128)(2,1)S(1)} all-gather(bf16[16,2048]{1,0:T(8,128)(2,1)S(1)} %get-tuple-element.276), channel_id=1, replica_groups=mesh['groups'=2,'seq'=32,'head'=8] {'head'}, dimensions={0}, use_global_device_ids=true | all-gather | bytes 589824 | tf_op jit(solution)/shard_map/all_gather | solution.py:204
  556.4 112.8 %all-gather.9.cloned.1.call-done = bf16[4096,512]{1,0:T(8,128)(2,1)} async-done(((bf16[128,512]{1,0:T(8,128)(2,1)}), bf16[4096,512]{1,0:T(8,128)(2,1)}) %all-gather.9.cloned.1.call-update) | async-done | bytes 4194320 | tf_op jit(solution)/shard_map/all_gather | solution.py:59
  669.2 4.5 fusion.113
  673.7 6.3 conditional.2
  674.6 2.5 fusion.111
  677.1 2.2 fusion.2
  680.2 6.4 conditional.3
  681.2 2.5 fusion.112
  683.7 2.2 fusion.15
  (205 shorter events, 72.9 us)
Async XLA Ops:
  7.2 439.0 %copy-start = (bf16[512,2048]{1,0:T(8,128)(2,1)S(1)}, bf16[512,2048]{1,0:T(8,128)(2,1)}, u32[]{:S(2)}) copy-start(bf16[512,2048]{1,0:T(8,128)(2,1)} %param.38) | copy-start | bytes 6291460
  7.2 57.4 %copy-start.8 = (bf16[128,512]{1,0:T(8,128)(2,1)S(1)}, bf16[128,512]{1,0:T(8,128)(2,1)}, u32[]{:S(2)}) copy-start(bf16[128,512]{1,0:T(8,128)(2,1)} %param.28) | copy-start | bytes 393220
  7.2 243.9 %all-gather.11.cloned.1.call-start = ((), (), s32[]{:S(2)}) async-start(), calls=%async_computation.3 | async-start | bytes 8650752 | tf_op jit(solution)/shard_map/all_gather | solution.py:27
  8.1 15.0 %collective-permute-start.1 = (bf16[3,256]{1,0:T(4,128)(2,1)S(1)}, bf16[3,256]{1,0:T(4,128)(2,1)S(1)}, u32[]{:S(2)}, u32[]{:S(2)}) collective-permute-start(bf16[3,256]{1,0:T(4,128)(2,1)S(1)} %slice.146), channel_id=1, source_target_pairs={{0,8},{8,16},{16,24},{24,32},{32,40},{40,48},{48,56},{56,64},{64,7... | collective-permute-start | bytes 4616 | tf_op jit(solution)/shard_map/ppermute | solution.py:22
  13.5 51.1 %collective-permute-start.2 = (bf16[3,512]{1,0:T(4,128)(2,1)S(1)}, bf16[3,512]{1,0:T(4,128)(2,1)S(1)}, u32[]{:S(2)}, u32[]{:S(2)}) collective-permute-start(bf16[3,512]{1,0:T(4,128)(2,1)S(1)} %slice.155), channel_id=1, source_target_pairs={{0,8},{8,16},{16,24},{24,32},{32,40},{40,48},{48,56},{56,64},{64,7... | collective-permute-start | bytes 9224 | tf_op jit(solution)/shard_map/ppermute | solution.py:22
  24.6 43.0 %copy-start.4 = (f32[128,2,2,128]{3,0,2,1:T(8,128)}, f32[128,2,2,128]{3,0,2,1:T(8,128)S(1)}, u32[]{:S(2)}) copy-start(f32[128,2,2,128]{3,0,2,1:T(8,128)S(1)} %broadcast_in_dim.123) | copy-start | bytes 786436
  65.8 3.0 copy-start.6
  68.8 16.5 %copy-start.9 = (bf16[64,1024]{1,0:T(8,128)(2,1)S(1)}, bf16[64,1024]{1,0:T(8,128)(2,1)}, u32[]{:S(2)}) copy-start(bf16[64,1024]{1,0:T(8,128)(2,1)} %param.40) | copy-start | bytes 393220
  71.1 1.9 copy-start.2
  75.3 1.9 copy-start.2
  77.2 0.7 copy-start.1
  77.2 0.8 copy-start.3
  77.2 12.5 %copy-start.5 = (f32[128,2,2,128]{3,0,2,1:T(8,128)S(1)}, f32[128,2,2,128]{3,0,2,1:T(8,128)}, u32[]{:S(2)}) copy-start(f32[128,2,2,128]{3,0,2,1:T(8,128)} %copy-done.4) | copy-start | bytes 786436
  78.0 317.0 %all-gather.13.cloned.1.call-start = ((), (), s32[]{:S(2)}) async-start(), calls=%async_computation.4 | async-start | bytes 8650752 | tf_op jit(solution)/shard_map/all_gather | solution.py:27
  78.8 11.5 %copy-start.7 = (f32[2,4,64,256]{3,2,1,0:T(8,128)S(1)}, f32[2,4,64,256]{3,2,1,0:T(8,128)}, u32[]{:S(2)}) copy-start(f32[2,4,64,256]{3,2,1,0:T(8,128)} %copy-done.6) | copy-start | bytes 1572868
  78.8 455.3 %all-gather.7.cloned.1.call-start = ((), (), s32[]{:S(2)}) async-start(), calls=%async_computation.1 | async-start | bytes 6488064 | tf_op jit(solution)/shard_map/all_gather | solution.py:59
  79.6 8.5 %collective-permute-start = (bf16[3,256]{1,0:T(4,128)(2,1)S(1)}, bf16[3,256]{1,0:T(4,128)(2,1)S(1)}, u32[]{:S(2)}, u32[]{:S(2)}) collective-permute-start(bf16[3,256]{1,0:T(4,128)(2,1)S(1)} %slice.137), channel_id=1, source_target_pairs={{0,8},{8,16},{16,24},{24,32},{32,40},{40,48},{48,56},{56,64},{64,7... | collective-permute-start | bytes 4616 | tf_op jit(solution)/shard_map/ppermute | solution.py:22
  442.5 3.6 copy-start.10
  442.5 3.6 copy-start.11
  447.7 19.9 %copy-start.12 = (f32[2048]{0:T(1024)S(1)}, f32[2048]{0:T(1024)}, u32[]{:S(2)}) copy-start(f32[2048]{0:T(1024)} %param.39) | copy-start | bytes 24580
  447.7 18.8 %all-to-all-start = ((f32[8,16,2048]{2,1,0:T(8,128)}), f32[8,16,2048]{2,1,0:T(8,128)S(1)}, u32[]{:S(2)}, u32[]{:S(2)}) async-start(f32[8,16,2048]{2,1,0:T(8,128)} %fusion.49), calls=%async_computation | async-start | bytes 2097152 | tf_op jit(solution)/shard_map/all_to_all | solution.py:49
  452.6 216.6 %all-gather.9.cloned.1.call-start = ((), (), s32[]{:S(2)}) async-start(), calls=%async_computation.2 | async-start | bytes 4325376 | tf_op jit(solution)/shard_map/all_gather | solution.py:59
Sparse Core Ops, SparseCore 0:
  78.1 172.9 all-gather.10
  253.2 141.7 all-gather.12
  397.1 136.9 all-gather.6
  536.9 132.1 all-gather.8
where the time goes:
time: 697 us; the launch traced here: 695 us
  waiting for transfers between devices  485 us (70%)
  matrix products  76.7 us (11%)
  other arithmetic  50.1 us (7%)
  blocking collectives  26.3 us (4%)
  local copies, waits for them, and re-layouts  20 us (3%)
  starting transfers between devices  19.4 us (3%)
  between operations  16.4 us (2%)
    all_gather x2, waiting for transfers between devices, entering_2(): everything = jax.tree.map(lambda part: lax.all_gather(part, axis), shard)  304 us
    all_gather x2, waiting for transfers between devices, in_one_piece(): lax.all_gather(both, axis, axis=dim, tiled=True)  166 us
    dot_general x34, matrix products, compose_pair(): jnp.einsum('auf,afi->aui', later_rows[0], earlier_rows[1], precision=high...  49.8 us
    another operation x3, other arithmetic, span_terms(): jax.scipy.linalg.solve_triangular(lower_part, right_side, lower=True, uni...  39.3 us
    ppermute x3, starting transfers between devices, shifted(): return lax.ppermute(shard, axis, pairs)  14.3 us
  transfers between devices with their start and end apart: 8, of which 5 were waited for; matrix products, arithmetic and copies ran while one was open for 16% of the time, Pallas kernels for 0%

commit v1 on v0

v1 whole, which is shorter than its diff:
```python
import functools

import jax
import jax.numpy as jnp
from jax import lax
from jax.experimental import pallas as pl
from jax.experimental.pallas import tpu as pltpu
from jax.sharding import PartitionSpec as P

DK = 128
DV = 128
QUERY_HEADS = 16
KEY_VALUE_HEADS = 2
HEAD_WIDTH = 256
CONV = 4
EPSILON = 1e-06
NEGATIVE = -1e30
MESH = pl.DeviceIdType.MESH
BF = jnp.bfloat16
F32 = jnp.float32


def dot(a, b):
    return lax.dot_general(a, b, (((1,), (0,)), ((), ())), preferred_element_type=F32)


def dot_t(a, b):
    return lax.dot_general(a, b, (((1,), (1,)), ((), ())), preferred_element_type=F32)


def halves(a):
    high = a.astype(BF)
    return high, (a - high.astype(F32)).astype(BF)


def fine(a, b, mul=dot):
    ah, al = halves(a)
    bh, bl = halves(b)
    return mul(ah, bh) + (mul(ah, bl) + mul(al, bh))


def fine_left(a, b):
    ah, al = halves(a)
    return dot(ah, b) + dot(al, b)


def silu(x):
    return x / (1.0 + jnp.exp(-x))


def sigmoid(x):
    return 1.0 / (1.0 + jnp.exp(-x))


def softplus(x):
    u = jnp.exp(-jnp.abs(x))
    series = u * (1.0 - u * (0.5 - u * (1.0 / 3.0 - u * 0.25)))
    return jnp.maximum(x, 0.0) + jnp.where(u < 0.01, series, jnp.log(1.0 + u))


class Copy:
    def __init__(self, src, dst, send, recv, **where):
        self.copy = pltpu.make_async_remote_copy(
            src_ref=src, dst_ref=dst, send_sem=send, recv_sem=recv, device_id=where, device_id_type=MESH
        )

    def start(self):
        self.copy.start()

    def sent(self):
        self.copy.wait_send()

    def came(self):
        self.copy.wait_recv()


def kernel(
    NS,
    NH,
    residual,
    query_in,
    key_in,
    value_in,
    gating_in,
    beta_logit,
    decay_logit,
    seq_length,
    conv_query,
    conv_key,
    conv_value,
    decay_rate,
    norm_gain,
    out_weight,
    attn_gain,
    query_weight,
    key_value_weight,
    hidden_out,
    attention_out,
    qkv,
    halo,
    xp,
    gating,
    res,
    wout,
    wq,
    wkv,
    pair,
    in1,
    blk,
    in_r,
    in_l,
    pre,
    s_out,
    s_in,
    w_mat,
    u_mat,
    q_mat,
    a_mat,
    gated,
    part,
    pbuf,
    pin,
    hid,
    normed,
    kv,
    q_att,
    g_att,
    peak,
    total,
    accum,
    local,
    halo_s,
    halo_r,
    wq_s,
    wq_r,
    wkv_s,
    wkv_r,
    s1_s,
    s1_r,
    ag_s,
    ag_r,
    st_s,
    st_r,
    rs_s,
    rs_r,
    hg_s,
    hg_r,
    kr_s,
    kr_r,
    kl_s,
    kl_r,
    kx_s,
    kx_r,
):
    z = lax.axis_index("seq")
    h = lax.axis_index("head")
    rows = query_in.shape[0]
    kcols = query_in.shape[1]
    vcols = value_in.shape[1]
    heads = vcols // DV
    kheads = kcols // DK
    BLK = heads
    NB = NS // BLK
    b = z // BLK
    zl = z % BLK
    right = lax.rem(z + 1, NS)
    left = lax.rem(z + NS - 1, NS)
    far_r = lax.rem(z + BLK, NS)
    far_l = lax.rem(z + NS - BLK, NS)
    share = rows // NH
    core = h % 2
    other = h + 1 - 2 * core
    length = seq_length[0]
    wrows = query_weight.shape[0]

    barrier = pltpu.get_barrier_semaphore()

    def greet(**where):
        pl.semaphore_signal(barrier, inc=1, device_id=where, device_id_type=MESH)

    greet(seq=right)
    greet(seq=left)
    greet(seq=far_r)
    greet(seq=far_l)
    for d in range(1, BLK):
        greet(seq=b * BLK + lax.rem(zl + d, BLK))
    for d in range(1, NH):
        greet(head=lax.rem(h + d, NH))
    half = NS // 2
    early = half - 1

    @pl.when(z < early)
    def _():
        greet(seq=NS - 1)

    @pl.when(z == NS - 1)
    def _():
        for t in range(early):
            greet(seq=t)

    def fetch(i, src, dst):
        return pltpu.make_async_copy(src, dst, local.at[i])

    kvh = h // (NH // KEY_VALUE_HEADS)
    kv_start = pl.multiple_of((core * KEY_VALUE_HEADS + kvh) * HEAD_WIDTH, HEAD_WIDTH)
    fetches = [
        fetch(0, query_in, qkv.at[:, pl.ds(0, kcols)]),
        fetch(1, key_in, qkv.at[:, pl.ds(kcols, kcols)]),
        fetch(2, value_in, qkv.at[:, pl.ds(2 * kcols, vcols)]),
        fetch(3, query_weight, wq.at[pl.ds(pl.multiple_of(z * wrows, wrows), wrows)]),
        fetch(
            4,
            key_value_weight.at[:, pl.ds(kv_start, HEAD_WIDTH)],
            wkv.at[pl.ds(pl.multiple_of(z * wrows, wrows), wrows)],
        ),
        fetch(5, gating_in, gating),
        fetch(6, residual.at[pl.ds(pl.multiple_of(h * share, share), share)], res),
        fetch(7, out_weight, wout),
    ]
    for f in fetches:
        f.start()
    for f in fetches[:5]:
        f.wait()
    peers = 4 + (BLK - 1) + (NH - 1)
    pl.semaphore_wait(barrier, peers + jnp.where(z < early, 1, 0) + jnp.where(z == NS - 1, early, 0))

    halo_copy = Copy(qkv.at[pl.ds(rows - 16, 16)], halo, halo_s, halo_r, seq=right)
    halo_copy.start()

    steps_r, steps_l = NS // 2, (NS - 1) // 2

    def weight_copies(d, s):
        tile = lax.rem(z + NS - (s - 1), NS) if d == 0 else lax.rem(z + (s - 1), NS)
        at = pl.ds(pl.multiple_of(tile * wrows, wrows), wrows)
        to = right if d == 0 else left
        return (
            Copy(wkv.at[at], wkv.at[at], wkv_s.at[d, s - 1], wkv_r.at[d, s - 1], seq=to),
            Copy(wq.at[at], wq.at[at], wq_s.at[d, s - 1], wq_r.at[d, s - 1], seq=to),
        )

    def pump(s):
        for d, steps in ((0, steps_r), (1, steps_l)):
            if s > 1 and s - 1 <= steps:
                for c in weight_copies(d, s - 1):
                    c.came()
            if s <= steps:
                for c in weight_copies(d, s):
                    c.start()

    pump(1)

    halo_copy.came()
    tail = halo[...].astype(F32)[8:16]
    xp[0:8, :] = jnp.where(z > 0, tail, 0.0)
    xp[8 : 8 + rows, :] = qkv[...].astype(F32)

    def conv(taps, start, width):
        acc = jnp.zeros((rows, width), F32)
        for j in range(CONV):
            acc = acc + taps[j : j + 1, :] * xp[9 - CONV + j : 9 - CONV + j + rows, start : start + width]
        return silu(acc)

    def unit(x):
        return x * lax.rsqrt(jnp.sum(x * x, -1, keepdims=True) + EPSILON)

    qs = [unit(conv(conv_query[:, i * DK : (i + 1) * DK], i * DK, DK)) * DK**-0.5 for i in range(kheads)]
    ks = [unit(conv(conv_key[:, i * DK : (i + 1) * DK], kcols + i * DK, DK)) for i in range(kheads)]

    position = z * rows + lax.broadcasted_iota(jnp.int32, (rows, heads), 0)
    alive = (position < length).astype(F32)
    betas = sigmoid(beta_logit[...]) * alive
    log_decay = -decay_rate[...] * softplus(decay_logit[...]) * alive
    ri = lax.broadcasted_iota(jnp.int32, (rows, rows), 0)
    ci = lax.broadcasted_iota(jnp.int32, (rows, rows), 1)
    inclusive = ri >= ci
    strict = ri > ci
    tril = jnp.where(inclusive, 1.0, 0.0).astype(BF)
    pump(2)
    grams = [fine(k, k, dot_t) for k in ks]
    mixes = [fine(q, k, dot_t) for q, k in zip(qs, ks)]
    lowers, rights, kds, ends = [], [], [], []
    for v in range(heads):
        j = v * kheads // heads
        g = jnp.broadcast_to(log_decay[:, v : v + 1], (rows, rows))
        g1 = g.astype(BF)
        rest = g - g1.astype(F32)
        g2 = rest.astype(BF)
        g3 = (rest - g2.astype(F32)).astype(BF)
        run = dot(tril, g1) + (dot(tril, g2) + dot(tril, g3))
        spread = run - run.T
        within = jnp.where(inclusive, jnp.exp(jnp.where(inclusive, spread, 0.0)), 0.0)
        grow = jnp.exp(run)
        beta = betas[:, v : v + 1]
        lowers.append(jnp.where(strict, beta * within * grams[j], 0.0))
        value = conv(conv_value[:, v * DV : (v + 1) * DV], 2 * kcols + v * DV, DV)
        rights.append((beta * grow * ks[j], beta * value))
        end = run[rows - 1 : rows, :]
        kds.append((jnp.exp(end - run) * ks[j]).T)
        ends.append(jnp.exp(end))
        a_mat[v] = mixes[j] * within
        q_mat[v] = grow * qs[j]
    pump(3)
    eye = jnp.where(ri == ci, 1.0, 0.0)
    inverses = []
    for v in range(heads):
        inverses.append(eye - jnp.where((ri // 2 == ci // 2), lowers[v], 0.0))
    size = 2
    while size < rows:
        mask = (ri // (2 * size) == ci // (2 * size)) & (ri // size != ci // size)
        steps = [fine(jnp.where(mask, lowers[v], 0.0), inverses[v]) for v in range(heads)]
        inverses = [inverses[v] - fine(inverses[v], steps[v]) for v in range(heads)]
        size *= 2
    pump(4)
    for v in range(heads):
        solved = fine(inverses[v], jnp.concatenate(rights[v], 1))
        w_mat[v] = solved[:, :DK]
        u_mat[v] = solved[:, DK:]
        both = fine(kds[v], solved)
        pair[v, :, :DK] = (jnp.where(ri == ci, ends[v], 0.0) - both[:, :DK]).astype(BF)
        pair[v, :, DK:] = both[:, DK:].astype(BF)
    stage = []
    for d in range(1, BLK):
        to = lax.rem(zl + d, BLK)
        stage.append(Copy(pair.at[to], in1.at[zl], s1_s.at[d], s1_r.at[zl], seq=b * BLK + to))
        stage[-1].start()
    in1[zl] = pair[zl]
    pump(5)
    for d in range(1, BLK):
        frm = lax.rem(zl + d, BLK)
        Copy(in1.at[frm], in1.at[frm], s1_s.at[d], s1_r.at[frm], seq=right).came()
    running = in1[0].astype(F32)
    for i in range(1, BLK):
        pre[i] = running
        running = fine_right(in1[i][:, :DK], running)
        running = jnp.concatenate([running[:, :DK], running[:, DK:] + in1[i][:, DK:].astype(F32)], 1)
    blk[...] = running.astype(BF)
    ag_steps = (NB // 2, (NB - 1) // 2)
    CH = ag_s.shape[2]
    crow = DK // CH

    def ag_copy(d, s, k):
        at = pl.ds(k * crow, crow)
        buf = (in_r, in_l)[d]
        src = blk.at[at] if s == 1 else buf.at[s - 2, at]
        return Copy(
            src, buf.at[s - 1, at], ag_s.at[d, s - 1, k], ag_r.at[d, s - 1, k], seq=(far_r, far_l)[d]
        )

    for k in range(CH):
        for d in range(2):
            ag_copy(d, 1, k).start()
    pump(6)
    near_t = eye
    near_i = jnp.zeros((DK, DV), F32)
    far = jnp.zeros((DK, DV), F32)
    for s in range(1, ag_steps[0] + 1):
        for k in range(CH):
            for d in range(2):
                if s <= ag_steps[d]:
                    ag_copy(d, s, k).came()
                    if s + 1 <= ag_steps[d]:
                        ag_copy(d, s + 1, k).start()
        pump(6 + s)
        prod = fine_left(near_t, in_r[s - 1])
        ok = b - s >= 0
        near_i = jnp.where(ok, near_i + prod[:, DK:], near_i)
        near_t = jnp.where(ok, prod[:, :DK], near_t)
        if s <= ag_steps[1]:
            item = in_l[s - 1]
            nxt = fine_right(item[:, :DK], far) + item[:, DK:].astype(F32)
            far = jnp.where(b + s >= NB, nxt, far)
    entering = near_i + fine(near_t, far)
    done = 6 + ag_steps[0]
    s_out[0] = entering.astype(BF)
    for i in range(1, BLK):
        s_out[i] = (fine(pre[i][:, :DK], entering) + pre[i][:, DK:]).astype(BF)
    states = []
    for d in range(1, BLK):
        to = lax.rem(zl + d, BLK)
        states.append(Copy(s_out.at[to], s_in.at[zl], st_s.at[d], st_r.at[zl], seq=b * BLK + to))
        states[-1].start()
    s_in[zl] = s_out[zl]
    pump(done + 1)
    for d in range(1, BLK):
        frm = lax.rem(zl + d, BLK)
        Copy(s_in.at[frm], s_in.at[frm], st_s.at[d], st_r.at[frm], seq=right).came()

    for f in fetches[5:]:
        f.wait()
    for v in range(heads):
        lhs = jnp.concatenate([w_mat[v], q_mat[v]], 0)
        both = fine_left(lhs, s_in[v])
        delta = u_mat[v] - both[:rows]
        o = both[rows:] + fine(a_mat[v], delta)
        o = o * lax.rsqrt(jnp.mean(o * o, -1, keepdims=True) + EPSILON) * norm_gain[...]
        gate = silu(gating[:, v * DV : (v + 1) * DV].astype(F32))
        gated[:, v * DV : (v + 1) * DV] = (o * gate).astype(BF)
    width = wout.shape[1]
    strip = 512
    for n in range(0, width, strip):
        piece = dot(gated[...], wout[:, n : n + strip])
        part[:, n : n + strip] = piece
        pbuf[:, n : n + strip] = piece.astype(BF)
    mine = pl.ds(pl.multiple_of(h * share, share), share)

    def strip_of(i):
        return pl.ds(pl.multiple_of(i * share, share), share)

    sums = []
    for d in range(1, NH):
        to = lax.rem(h + d, NH)
        sums.append(Copy(pbuf.at[strip_of(to)], pin.at[h], rs_s.at[d], rs_r.at[h], head=to))
        sums[-1].start()
    pump(done + 2)
    acc = part[mine, :] + res[...].astype(F32)
    for d in range(1, NH):
        frm = lax.rem(h + d, NH)
        Copy(pin.at[frm], pin.at[frm], rs_s.at[d], rs_r.at[frm], head=frm).came()
        acc = acc + pin[frm].astype(F32)
    hid[mine, :] = acc.astype(BF)
    gathers = []
    for d in range(1, NH):
        to = lax.rem(h + d, NH)
        gathers.append(Copy(hid.at[mine], hid.at[mine], hg_s.at[d], hg_r.at[h], head=to))
        gathers[-1].start()
    pump(done + 3)
    for d in range(1, NH):
        frm = lax.rem(h + d, NH)
        Copy(hid.at[strip_of(frm)], hid.at[strip_of(frm)], hg_s.at[d], hg_r.at[frm], head=frm).came()
    save = pltpu.make_async_copy(hid, hidden_out, local.at[8])
    save.start()
    for n in range(0, rows, 32):
        x = hid[n : n + 32, :].astype(F32)
        x = x * lax.rsqrt(jnp.mean(x * x, -1, keepdims=True) + EPSILON) * attn_gain[...]
        normed[n : n + 32, :] = x.astype(BF)
    for s in range(done + 4, steps_r + 2):
        pump(s)

    kv[core, z] = dot(normed[...], wkv[...]).astype(BF)

    def kr_copy(s):
        item = z - (s - 1)
        return Copy(kv.at[core, item], kv.at[core, item], kr_s.at[s - 1], kr_r.at[s - 1], seq=right)

    def kl_copy(i):
        return Copy(kv.at[core, i], kv.at[core, i], kl_s.at[i], kl_r.at[i], seq=left)

    def kx_copy(i):
        return Copy(kv.at[core, i], kv.at[core, i], kx_s.at[i], kx_r.at[i], head=other)

    def kx_came(i):
        return Copy(kv.at[1 - core, i], kv.at[1 - core, i], kx_s.at[i], kx_r.at[i], head=other)

    @pl.when(z < NS - 1)
    def _():
        kr_copy(1).start()

    kx_copy(z).start()
    direct = Copy(kv.at[core, z], kv.at[core, z], kl_s.at[early], kl_r.at[z], seq=NS - 1)

    @pl.when(z < early)
    def _():
        direct.start()

    qrows = wq.shape[1] // (2 * HEAD_WIDTH)
    for i in range(qrows):
        at = 2 * i * HEAD_WIDTH
        q_att[i * rows : (i + 1) * rows, :] = (
            dot(normed[...], wq[:, at : at + HEAD_WIDTH]) * HEAD_WIDTH**-0.5
        ).astype(BF)
        g_att[i * rows : (i + 1) * rows, :] = dot(normed[...], wq[:, at + HEAD_WIDTH : at + 2 * HEAD_WIDTH])

    peak[...] = jnp.full(peak.shape, NEGATIVE, F32)
    total[...] = jnp.zeros(total.shape, F32)
    accum[...] = jnp.zeros(accum.shape, F32)

    def attend(item):
        scores = dot_t(q_att[...], kv[0, item])
        n = qrows * rows
        qpos = z * rows + lax.broadcasted_iota(jnp.int32, (n, rows), 0) % rows
        kpos = item * rows + lax.broadcasted_iota(jnp.int32, (n, rows), 1)
        visible = (kpos <= qpos) & (kpos < length)
        scores = jnp.where(visible, scores, NEGATIVE)
        old = peak[:, 0:1]
        new = jnp.maximum(old, jnp.max(scores, -1, keepdims=True))
        weights = jnp.where(visible, jnp.exp(scores - new), 0.0)
        scale = jnp.exp(old - new)
        peak[...] = jnp.broadcast_to(new, peak.shape)
        total[...] = total[...] * scale + jnp.sum(weights, -1, keepdims=True)
        accum[...] = accum[...] * scale + dot(weights.astype(BF), kv[1, item])

    kx_came(z).came()
    attend(z)

    @pl.loop(1, half + 1)
    def _(s):
        @pl.when(z - s >= 0)
        def _():
            item = z - s
            Copy(kv.at[core, item], kv.at[core, item], kr_s.at[s - 1], kr_r.at[s - 1], seq=right).came()

            @pl.when((s < half) & (z < NS - 1))
            def _():
                kr_copy(s + 1).start()

            kx_copy(item).start()

        i = s - 1

        @pl.when(i <= z - half - 1)
        def _():
            Copy(kv.at[core, i], kv.at[core, i], kl_s.at[i], kl_r.at[i], seq=left).came()

            @pl.when(i <= z - half - 2)
            def _():
                kl_copy(i).start()

            kx_copy(i).start()

        @pl.when(z - s >= 0)
        def _():
            kx_came(z - s).came()
            attend(z - s)

        @pl.when(i <= z - half - 1)
        def _():
            kx_came(i).came()
            attend(i)

    for i in range(qrows):
        at = slice(i * rows, (i + 1) * rows)
        o = accum[at, :] / total[at, 0:1] * sigmoid(g_att[at, :])
        attention_out[:, i * HEAD_WIDTH : (i + 1) * HEAD_WIDTH] = o.astype(BF)

    save.wait()
    halo_copy.sent()
    for d, steps in ((0, steps_r), (1, steps_l)):
        for s in range(1, steps + 1):
            for c in weight_copies(d, s):
                c.sent()
            for k in range(CH):
                if s <= ag_steps[d]:
                    ag_copy(d, s, k).sent()
    for c in stage + states + sums + gathers:
        c.sent()

    @pl.when(z < early)
    def _():
        direct.sent()

    @pl.loop(1, half + 1)
    def _(s):
        @pl.when((z - s + 1 >= 0) & (z < NS - 1))
        def _():
            kr_copy(s).sent()

        @pl.when(s - 1 <= z - half - 2)
        def _():
            kl_copy(s - 1).sent()

    @pl.loop(0, z + 1)
    def _(i):
        kx_copy(i).sent()


def fine_right(a, b):
    bh, bl = halves(b)
    return dot(a, bh) + dot(a, bl)


def shards(NS, NH, *args):
    (
        residual,
        query_in,
        key_in,
        value_in,
        gating_in,
        beta_logit,
        decay_logit,
        seq_length,
        conv_query,
        conv_key,
        conv_value,
        decay_rate,
        norm_gain,
        out_weight,
        attn_gain,
        query_weight,
        key_value_weight,
    ) = args
    rows, model = residual.shape
    kcols, vcols = query_in.shape[1], value_in.shape[1]
    heads = vcols // DV
    wcols = query_weight.shape[1]
    qheads = wcols // (2 * HEAD_WIDTH)
    nb = NS // heads
    half = NS // 2
    share = rows // NH
    ch = 4
    hbm = pl.BlockSpec(memory_space=pl.ANY)
    vmem = pl.BlockSpec(memory_space=pltpu.VMEM)
    smem = pl.BlockSpec(memory_space=pltpu.SMEM)
    dma = pltpu.SemaphoreType.DMA
    V = pltpu.VMEM
    scratch = [
        V((rows, 2 * kcols + vcols), BF),
        V((16, 2 * kcols + vcols), BF),
        V((rows + 8, 2 * kcols + vcols), F32),
        V((rows, vcols), BF),
        V((share, model), BF),
        V(out_weight.shape, BF),
        V((model, wcols), BF),
        V((model, HEAD_WIDTH), BF),
        V((heads, DK, DK + DV), BF),
        V((heads, DK, DK + DV), BF),
        V((DK, DK + DV), BF),
        V((nb // 2, DK, DK + DV), BF),
        V(((nb - 1) // 2, DK, DK + DV), BF),
        V((heads, DK, DK + DV), F32),
        V((heads, DK, DV), BF),
        V((heads, DK, DV), BF),
        V((heads, rows, DK), F32),
        V((heads, rows, DV), F32),
        V((heads, rows, DK), F32),
        V((heads, rows, rows), F32),
        V((rows, vcols), BF),
        V((rows, model), F32),
        V((rows, model), BF),
        V((NH, share, model), BF),
        V((rows, model), BF),
        V((rows, model), BF),
        V((2, NS, rows, HEAD_WIDTH), BF),
        V((qheads * rows, HEAD_WIDTH), BF),
        V((qheads * rows, HEAD_WIDTH), F32),
        V((qheads * rows, 128), F32),
        V((qheads * rows, 128), F32),
        V((qheads * rows, HEAD_WIDTH), F32),
        dma((9,)),
        dma,
        dma,
        dma((2, half)),
        dma((2, half)),
        dma((2, half)),
        dma((2, half)),
        dma((heads,)),
        dma((heads,)),
        dma((2, nb // 2, ch)),
        dma((2, nb // 2, ch)),
        dma((heads,)),
        dma((heads,)),
        dma((NH,)),
        dma((NH,)),
        dma((NH,)),
        dma((NH,)),
        dma((half,)),
        dma((half,)),
        dma((half,)),
        dma((half,)),
        dma((NS,)),
        dma((NS,)),
    ]
    return pl.pallas_call(
        functools.partial(kernel, NS, NH),
        name="layer",
        out_shape=(
            jax.ShapeDtypeStruct((rows, model), BF),
            jax.ShapeDtypeStruct((rows, qheads * HEAD_WIDTH), BF),
        ),
        in_specs=[hbm, hbm, hbm, hbm, hbm, vmem, vmem, smem, vmem, vmem, vmem, vmem, vmem, hbm, vmem, hbm, hbm],
        out_specs=(hbm, vmem),
        scratch_shapes=scratch,
        compiler_params=pltpu.CompilerParams(
            collective_id=0, has_side_effects=True, vmem_limit_bytes=56 * 1024 * 1024
        ),
    )(
        residual,
        query_in,
        key_in,
        value_in,
        gating_in,
        beta_logit,
        decay_logit,
        seq_length,
        conv_query,
        conv_key,
        conv_value,
        decay_rate.reshape(1, -1),
        norm_gain.reshape(1, -1),
        out_weight,
        attn_gain.reshape(1, -1),
        query_weight,
        key_value_weight,
    )


def solution(mesh):
    placed = (
        P(("groups", "seq"), None),
        P(("groups", "seq"), "head"),
        P(("groups", "seq"), "head"),
        P(("groups", "seq"), "head"),
        P(("groups", "seq"), "head"),
        P(("groups", "seq"), "head"),
        P(("groups", "seq"), "head"),
        P("groups"),
        P(None, "head"),
        P(None, "head"),
        P(None, "head"),
        P("head"),
        P(),
        P("head", None),
        P(),
        P("seq", "head"),
        P("seq", None),
    )
    return jax.shard_map(
        functools.partial(shards, mesh.shape["seq"], mesh.shape["head"]),
        mesh=mesh,
        in_specs=placed,
        out_specs=(P(("groups", "seq"), None), P(("groups", "seq"), "head")),
        check_vma=False,
    )
```

time: 697 us -> 247 us (0.35)
  the two profiles are of different devices: /device:TPU:38 before, /device:TPU:4009 now
where the time goes in v1:
time: 247 us
  Pallas kernels  240 us (97%)
  local copies, waits for them, and re-layouts  6.28 us (3%)
    pallas_call x1, Pallas kernels, shards(): pl.pallas_call(functools.partial(kernel, NS, NH), name='layer', out_shape...  240 us
    unnamed x4, local copies, waits for them, and re-layouts  6.28 us

profile of v1, /device:TPU:4009, one launch (start us, length us, event | category | flops | bytes accessed | tf_op | source)
XLA Modules:
  0.0 247.1 jit_solution(13104131020396218691)
XLA Ops:
  1.3 1.4 copy.19.beta_logit
  2.7 1.4 copy.20.decay_logit
  4.1 239.6 %layer.1 = (bf16[128,2048]{1,0:T(8,128)(2,1)}, bf16[128,512]{1,0:T(8,128)(2,1)}) custom-call(bf16[128,2048]{1,0:T(8,128)(2,1)} %residual.1, bf16[128,256]{1,0:T(8,128)(2,1)} %query_in.1, bf16[128,256]{1,0:T(8,128)(2,1)} %key_in.1, bf16[128,512]{1,0:T(8,128)(2,1)} %value_in.1, bf16[128,512]{1,0:T(8,128)(2,1)} %gating_in.1, f32[128,4]{1,0:T(8,128)} %copy.19.beta_logit, ...), custom_call_target="tpu_custom_call" | custom-call | tf_op jit(solution)/shard_map/layer/pallas_call | solution.py:662
  243.7 1.9 copy.24
  245.6 1.6 copy.25

commit v2 on v1

v2 whole, which is shorter than its diff:
```python
import functools

import jax
import jax.numpy as jnp
from jax import lax
from jax.experimental import pallas as pl
from jax.experimental.pallas import tpu as pltpu
from jax.sharding import PartitionSpec as P

DK = 128
DV = 128
QUERY_HEADS = 16
KEY_VALUE_HEADS = 2
HEAD_WIDTH = 256
CONV = 4
PART = HEAD_WIDTH // 2
EPSILON = 1e-06
NEGATIVE = -1e30
MESH = pl.DeviceIdType.MESH
BF = jnp.bfloat16
F32 = jnp.float32


def dot(a, b):
    return lax.dot_general(a, b, (((1,), (0,)), ((), ())), preferred_element_type=F32)


def dot_t(a, b):
    return lax.dot_general(a, b, (((1,), (1,)), ((), ())), preferred_element_type=F32)


def halves(a):
    high = a.astype(BF)
    return high, (a - high.astype(F32)).astype(BF)


def fine(a, b, mul=dot):
    ah, al = halves(a)
    bh, bl = halves(b)
    return mul(ah, bh) + (mul(ah, bl) + mul(al, bh))


def fine_left(a, b):
    ah, al = halves(a)
    return dot(ah, b) + dot(al, b)


def silu(x):
    return x / (1.0 + jnp.exp(-x))


def sigmoid(x):
    return 1.0 / (1.0 + jnp.exp(-x))


def softplus(x):
    u = jnp.exp(-jnp.abs(x))
    series = u * (1.0 - u * (0.5 - u * (1.0 / 3.0 - u * 0.25)))
    return jnp.maximum(x, 0.0) + jnp.where(u < 0.01, series, jnp.log(1.0 + u))


class Copy:
    def __init__(self, src, dst, send, recv, **where):
        self.copy = pltpu.make_async_remote_copy(
            src_ref=src, dst_ref=dst, send_sem=send, recv_sem=recv, device_id=where, device_id_type=MESH
        )

    def start(self):
        self.copy.start()

    def sent(self):
        self.copy.wait_send()

    def came(self):
        self.copy.wait_recv()


def kernel(
    NG,
    NS,
    NH,
    residual,
    query_in,
    key_in,
    value_in,
    gating_in,
    beta_logit,
    decay_logit,
    seq_length,
    conv_query,
    conv_key,
    conv_value,
    decay_rate,
    norm_gain,
    out_weight,
    attn_gain,
    query_weight,
    key_value_weight,
    hidden_out,
    attention_out,
    qkv,
    halo,
    xp,
    gating,
    res,
    wout,
    wq,
    wkv,
    pair,
    in1,
    blk,
    in_r,
    in_l,
    pre,
    near,
    distant,
    s_out,
    s_in,
    w_mat,
    u_mat,
    q_mat,
    a_mat,
    gated,
    part,
    pbuf,
    pin,
    hid,
    normed,
    kv,
    q_att,
    g_att,
    peak,
    total,
    accum,
    local,
    halo_s,
    halo_r,
    wq_s,
    wq_r,
    wkv_s,
    wkv_r,
    wy_s,
    wy_r,
    s1_s,
    s1_r,
    ag_s,
    ag_r,
    st_s,
    st_r,
    rs_s,
    rs_r,
    hg_s,
    hg_r,
    kr_s,
    kr_r,
    kl_s,
    kl_r,
    kx_s,
    kx_r,
    from_left,
    from_right,
    row_in,
    row_known,
    last_known,
):
    z = lax.axis_index("seq")
    h = lax.axis_index("head")
    g = lax.axis_index("groups")
    rows = query_in.shape[0]
    kcols = query_in.shape[1]
    vcols = value_in.shape[1]
    heads = vcols // DV
    kheads = kcols // DK
    BLK = heads
    NB = NS // BLK
    b = z // BLK
    zl = z % BLK
    right = lax.rem(z + 1, NS)
    left = lax.rem(z + NS - 1, NS)
    far_r = lax.rem(z + BLK, NS)
    far_l = lax.rem(z + NS - BLK, NS)
    share = rows // NH
    core = h % 2
    other = h + 1 - 2 * core
    side = (h // 2) % 2
    across = h + 2 - 4 * side
    mine_q, twin_q = 2 * side + core, 2 * side + 1 - core
    across_q, last_q = 2 * (1 - side) + core, 2 * (1 - side) + 1 - core
    paired = NG % 2 == 0
    turn = g % 2 if paired else 0
    ally = g + 1 - 2 * turn
    length = seq_length[0]
    wrows = query_weight.shape[0]

    barrier = pltpu.get_barrier_semaphore()

    def greet(**where):
        pl.semaphore_signal(barrier, inc=1, device_id=where, device_id_type=MESH)

    hop_r = lax.rem(z + 2, NS)
    hop_l = lax.rem(z + NS - 2, NS)
    for to in (right, left, hop_r, hop_l):
        greet(seq=to)
    if paired:
        greet(groups=ally)
    odd = z % 2 == 1

    @pl.when(odd)
    def _():
        for d in range(1, NH):
            greet(head=lax.rem(h + d, NH))

    half = NS // 2
    early = half - 1
    wrapped = (NB - 1) // 2

    def fetch(i, src, dst):
        return pltpu.make_async_copy(src, dst, local.at[i])

    kvh = h // (NH // KEY_VALUE_HEADS)
    kv_start = pl.multiple_of((side * KEY_VALUE_HEADS + kvh) * HEAD_WIDTH + core * PART, PART)
    fetches = [
        fetch(0, query_in, qkv.at[:, pl.ds(0, kcols)]),
        fetch(1, key_in, qkv.at[:, pl.ds(kcols, kcols)]),
        fetch(2, value_in, qkv.at[:, pl.ds(2 * kcols, vcols)]),
        fetch(3, query_weight, wq.at[pl.ds(pl.multiple_of(z * wrows, wrows), wrows)]),
        fetch(
            4,
            key_value_weight.at[:, pl.ds(kv_start, PART)],
            wkv.at[pl.ds(pl.multiple_of(z * wrows, wrows), wrows)],
        ),
        fetch(5, gating_in, gating),
        fetch(6, residual.at[pl.ds(pl.multiple_of(h * share, share), share)], res),
        fetch(7, out_weight, wout),
    ]
    for f in fetches:
        f.start()
    for f in fetches[:5]:
        f.wait()
    pl.semaphore_wait(barrier, 4 + (1 if paired else 0) + jnp.where(odd, NH - 1, 0))

    def tell(sem, **where):
        pl.semaphore_signal(sem, inc=1, device_id=where, device_id_type=MESH)

    tell(from_left, seq=hop_r)
    tell(from_right, seq=hop_l)

    @pl.when(odd)
    def _():
        for d in range(1, NH):
            tell(row_in, head=lax.rem(h + d, NH))

    halo_copy = Copy(qkv.at[pl.ds(rows - 16, 16)], halo, halo_s, halo_r, seq=right)
    halo_copy.start()

    steps_r, steps_l = NS // 2, (NS - 1) // 2
    owners = 2 if paired else 1
    wide = wq.shape[1] // (2 * owners)

    def columns(stream, owner):
        return pl.ds(pl.multiple_of((owner * 2 + stream) * wide, wide), wide)

    def tile_rows(tile):
        return pl.ds(pl.multiple_of(tile * wrows, wrows), wrows)

    def tile_at(d, distance):
        return lax.rem(z + NS - distance, NS) if d == 0 else lax.rem(z + distance, NS)

    def weight_copies(stream, d, distance, hops):
        at = tile_rows(tile_at(d, distance))
        to = ((right, left), (hop_r, hop_l))[hops - 1][d]
        sem = distance + hops - 1
        refs = [(wq.at[at, columns(stream, turn)], wq_s.at[stream, d, sem], wq_r.at[stream, d, sem])]
        if stream == 0:
            refs.insert(0, (wkv.at[at], wkv_s.at[d, sem], wkv_r.at[d, sem]))
        return [Copy(ref, ref, send, recv, seq=to) for ref, send, recv in refs]

    def weight_came(stream, d, distance):
        at = tile_rows(tile_at(d, distance))
        sem = distance - 1
        if stream == 0:
            Copy(wkv.at[at], wkv.at[at], wkv_s.at[d, sem], wkv_r.at[d, sem], seq=right).came()
        ref = wq.at[at, columns(stream, turn)]
        Copy(ref, ref, wq_s.at[stream, d, sem], wq_r.at[stream, d, sem], seq=right).came()

    reach = (steps_r, steps_l)

    def weight_sends(stream, d, k):
        return [
            c for hops in (2, 1) if 2 * k + hops <= reach[d] for c in weight_copies(stream, d, 2 * k, hops)
        ]

    def ally_copy(stream, tile, owner=None):
        ref = wq.at[tile_rows(tile), columns(stream, turn if owner is None else owner)]
        return Copy(ref, ref, wy_s.at[stream, tile], wy_r.at[stream, tile], groups=ally)

    turns = [(stream, k) for k in range(NS // 4 + 1) for stream in range(2)]

    def pump(count):
        for stream, k in turns[:count]:
            for d in range(2):
                if 0 < 2 * k <= reach[d]:
                    weight_came(stream, d, 2 * k)
                for c in weight_sends(stream, d, k):
                    c.start()
            for d in range(2):
                if 0 < 2 * k - 1 <= reach[d]:
                    weight_came(stream, d, 2 * k - 1)
            for d in range(2):
                for distance in (2 * k - 1, 2 * k):
                    if 0 < distance <= reach[d] and paired:
                        ally_copy(stream, tile_at(d, distance)).start()
        del turns[:count]

    pump(2)

    @pl.when(z > 0)
    def _():
        halo_copy.came()
        xp[0:8, :] = halo[...].astype(F32)[8:16]

    @pl.when(z == 0)
    def _():
        xp[0:8, :] = jnp.zeros((8, xp.shape[1]), F32)

    xp[8 : 8 + rows, :] = qkv[...].astype(F32)

    def conv(taps, start, width):
        acc = jnp.zeros((rows, width), F32)
        for j in range(CONV):
            acc = acc + taps[j : j + 1, :] * xp[9 - CONV + j : 9 - CONV + j + rows, start : start + width]
        return silu(acc)

    def unit(x):
        return x * lax.rsqrt(jnp.sum(x * x, -1, keepdims=True) + EPSILON)

    qs = [unit(conv(conv_query[:, i * DK : (i + 1) * DK], i * DK, DK)) * DK**-0.5 for i in range(kheads)]
    ks = [unit(conv(conv_key[:, i * DK : (i + 1) * DK], kcols + i * DK, DK)) for i in range(kheads)]

    position = z * rows + lax.broadcasted_iota(jnp.int32, (heads, rows), 1)
    alive = (position < length).astype(F32)
    betas = sigmoid(beta_logit[...]) * alive
    log_decay = -decay_rate[...] * softplus(decay_logit[...]) * alive
    ri = lax.broadcasted_iota(jnp.int32, (rows, rows), 0)
    ci = lax.broadcasted_iota(jnp.int32, (rows, rows), 1)
    inclusive = ri >= ci
    strict = ri > ci
    triu = jnp.where(ri <= ci, 1.0, 0.0).astype(BF)
    g1 = log_decay.astype(BF)
    rest = log_decay - g1.astype(F32)
    g2 = rest.astype(BF)
    g3 = (rest - g2.astype(F32)).astype(BF)
    runs = dot(g1, triu) + (dot(g2, triu) + dot(g3, triu))
    grams = [fine(k, k, dot_t) for k in ks]
    mixes = [fine(q, k, dot_t) for q, k in zip(qs, ks)]
    lowers, rights, kds, ends = [], [], [], []
    for v in range(heads):
        j = v * kheads // heads
        row = jnp.broadcast_to(runs[v : v + 1, :], (rows, rows))
        run = row.T
        spread = run - row
        within = jnp.where(inclusive, jnp.exp(jnp.where(inclusive, spread, 0.0)), 0.0)
        grow = jnp.exp(run)
        beta = jnp.broadcast_to(betas[v : v + 1, :], (rows, rows)).T
        lowers.append(jnp.where(strict, beta * within * grams[j], 0.0))
        value = conv(conv_value[:, v * DV : (v + 1) * DV], 2 * kcols + v * DV, DV)
        rights.append((beta * grow * ks[j], beta * value))
        end = run[rows - 1 : rows, :]
        kds.append((jnp.exp(end - run) * ks[j]).T)
        ends.append(jnp.exp(end))
        a_mat[v] = mixes[j] * within
        q_mat[v] = grow * qs[j]
    eye = jnp.where(ri == ci, 1.0, 0.0)
    inverses = []
    for v in range(heads):
        inverses.append(eye - jnp.where((ri // 2 == ci // 2), lowers[v], 0.0))
    size = 2
    while size < rows:
        mask = (ri // (2 * size) == ci // (2 * size)) & (ri // size != ci // size)
        steps = [fine(jnp.where(mask, lowers[v], 0.0), inverses[v]) for v in range(heads)]
        inverses = [inverses[v] - fine(inverses[v], steps[v]) for v in range(heads)]
        size *= 2
    for v in range(heads):
        solved = fine(inverses[v], jnp.concatenate(rights[v], 1))
        w_mat[v] = solved[:, :DK]
        u_mat[v] = solved[:, DK:]
        both = fine(kds[v], solved)
        pair[v, :, :DK] = (jnp.where(ri == ci, ends[v], 0.0) - both[:, :DK]).astype(BF)
        pair[v, :, DK:] = both[:, DK:].astype(BF)
    pl.semaphore_wait(from_right, 1)
    last_in_block = zl == BLK - 1

    @pl.when(last_in_block)
    def _():
        pl.semaphore_wait(from_left, 1)

    stage = []
    for d in range(1, BLK):
        to = lax.rem(zl + d, BLK)
        stage.append(Copy(pair.at[to], in1.at[zl], s1_s.at[d], s1_r.at[zl], seq=b * BLK + to))
        stage[-1].start()
    in1[zl] = pair[zl]
    pump(2)
    for d in range(1, BLK):
        frm = lax.rem(zl + d, BLK)
        Copy(in1.at[frm], in1.at[frm], s1_s.at[d], s1_r.at[frm], seq=right).came()
    running = in1[0].astype(F32)
    for i in range(1, BLK):
        pre[i] = running
        running = fine_right(in1[i][:, :DK], running)
        running = jnp.concatenate([running[:, :DK], running[:, DK:] + in1[i][:, DK:].astype(F32)], 1)
    blk[...] = running.astype(BF)
    ahead = NB // 2
    CH = ag_s.shape[2]
    crow = DK // CH

    def ag_copy(buf, src, d, slot, k, to):
        at = pl.ds(k * crow, crow)
        return Copy(src.at[at], buf.at[slot, at], ag_s.at[d, slot, k], ag_r.at[d, slot, k], seq=to)

    def ag_right(s, k):
        return ag_copy(in_r, blk if s == 1 else in_r.at[s - 2], 0, s - 1, k, far_r)

    def ag_left(s, k):
        return ag_copy(in_l, blk if s == 1 else in_l.at[s - 2], 1, s - 1, k, far_l)

    def goes_right(s):
        return (b >= s - 1) & (b < NB - 1)

    def left_at(place, s):
        return (place + s >= NB) | (place + s < wrapped)

    def goes_left(s):
        return left_at(lax.rem(b + NB - 1, NB), s)

    @pl.when(goes_right(1))
    def _():
        for k in range(CH):
            ag_right(1, k).start()

    @pl.when(jnp.logical_not(last_in_block))
    def _():
        pl.semaphore_wait(from_left, 1)

    @pl.when(goes_left(1))
    def _():
        for k in range(CH):
            ag_left(1, k).start()

    pump(2)
    eye2 = jnp.concatenate([eye, jnp.zeros((DK, DV), F32)], 1)
    near[...] = eye2
    distant[...] = jnp.zeros((DK, DV), F32)
    for s in range(1, ahead + 1):

        @pl.when(b >= s)
        def _(s=s):
            for k in range(CH):
                ag_right(s, k).came()
                if s < ahead:

                    @pl.when(goes_right(s + 1))
                    def _(k=k):
                        ag_right(s + 1, k).start()

        if s <= wrapped:

            @pl.when(left_at(b, s))
            def _(s=s):
                for k in range(CH):
                    ag_left(s, k).came()
                    if s < wrapped:

                        @pl.when(goes_left(s + 1))
                        def _(k=k):
                            ag_left(s + 1, k).start()

        pump(2)

        @pl.when(b >= s)
        def _(s=s):
            item = in_r[s - 1]
            if s == 1:
                near[...] = item.astype(F32)
            else:
                prod = fine_left(near[:, :DK], item)
                near[:, DK:] = near[:, DK:] + prod[:, DK:]
                near[:, :DK] = prod[:, :DK]

        if s <= wrapped:

            @pl.when(b + s >= NB)
            def _(s=s):
                item = in_l[s - 1]
                distant[...] = fine_right(item[:, :DK], distant[...]) + item[:, DK:].astype(F32)

    entering = near[:, DK:] + fine(near[:, :DK], distant[...])

    @pl.when(odd)
    def _():
        pl.semaphore_wait(row_in, NH - 1)
        tell(row_known, seq=left)

    @pl.when((z > 0) & (z < early))
    def _():
        pl.semaphore_wait(last_known, 1)

    @pl.when(z < early - 1)
    def _():
        tell(last_known, seq=right)

    s_out[0] = entering.astype(BF)
    for i in range(1, BLK):
        s_out[i] = (fine(pre[i][:, :DK], entering) + pre[i][:, DK:]).astype(BF)
    states = []
    for d in range(1, BLK):
        to = lax.rem(zl + d, BLK)
        states.append(Copy(s_out.at[to], s_in.at[zl], st_s.at[d], st_r.at[zl], seq=b * BLK + to))
        states[-1].start()
    s_in[zl] = s_out[zl]
    pump(1)
    for d in range(1, BLK):
        frm = lax.rem(zl + d, BLK)
        Copy(s_in.at[frm], s_in.at[frm], st_s.at[d], st_r.at[frm], seq=right).came()

    for f in fetches[5:]:
        f.wait()
    for v in range(heads):
        lhs = jnp.concatenate([w_mat[v], q_mat[v]], 0)
        both = fine_left(lhs, s_in[v])
        delta = u_mat[v] - both[:rows]
        o = both[rows:] + fine(a_mat[v], delta)
        o = o * lax.rsqrt(jnp.mean(o * o, -1, keepdims=True) + EPSILON) * norm_gain[...]
        gate = silu(gating[:, v * DV : (v + 1) * DV].astype(F32))
        gated[:, v * DV : (v + 1) * DV] = (o * gate).astype(BF)
    width = wout.shape[1]
    strip = 512
    for n in range(0, width, strip):
        piece = dot(gated[...], wout[:, n : n + strip])
        part[:, n : n + strip] = piece
        pbuf[:, n : n + strip] = piece.astype(BF)
    mine = pl.ds(pl.multiple_of(h * share, share), share)

    def strip_of(i):
        return pl.ds(pl.multiple_of(i * share, share), share)

    @pl.when(jnp.logical_not(odd))
    def _():
        pl.semaphore_wait(row_known, 1)

    sums = []
    for d in range(1, NH):
        to = lax.rem(h + d, NH)
        sums.append(Copy(pbuf.at[strip_of(to)], pin.at[h], rs_s.at[d], rs_r.at[h], head=to))
        sums[-1].start()
    pump(1)
    acc = part[mine, :] + res[...].astype(F32)
    for d in range(1, NH):
        frm = lax.rem(h + d, NH)
        Copy(pin.at[frm], pin.at[frm], rs_s.at[d], rs_r.at[frm], head=frm).came()
        acc = acc + pin[frm].astype(F32)
    hid[mine, :] = acc.astype(BF)
    gathers = []
    for d in range(1, NH):
        to = lax.rem(h + d, NH)
        gathers.append(Copy(hid.at[mine], hid.at[mine], hg_s.at[d], hg_r.at[h], head=to))
        gathers[-1].start()
    pump(2)
    for d in range(1, NH):
        frm = lax.rem(h + d, NH)
        Copy(hid.at[strip_of(frm)], hid.at[strip_of(frm)], hg_s.at[d], hg_r.at[frm], head=frm).came()
    save = pltpu.make_async_copy(hid, hidden_out, local.at[8])
    save.start()
    for n in range(0, rows, 32):
        x = hid[n : n + 32, :].astype(F32)
        x = x * lax.rsqrt(jnp.mean(x * x, -1, keepdims=True) + EPSILON) * attn_gain[...]
        normed[n : n + 32, :] = x.astype(BF)
    pump(len(turns))

    kv[mine_q, z] = dot(normed[...], wkv[...]).astype(BF)

    def item_copy(i, sends, recvs, at_send, at_recv, **where):
        return Copy(kv.at[mine_q, i], kv.at[mine_q, i], sends.at[at_send], recvs.at[at_recv], **where)

    def kr_near(k):
        return item_copy(z - 2 * k, kr_s, kr_r, 2 * k, 2 * k, seq=right)

    def kr_far(k):
        return item_copy(z - 2 * k, kr_s, kr_r, 2 * k + 1, 2 * k + 1, seq=hop_r)

    def kr_sends(k):
        have = (z >= 2 * k) & (2 * k < half)
        return have & (z < NS - 2), have & (z < NS - 1)

    def kl_near(i):
        return item_copy(i, kl_s, kl_r, 2 * i, i, seq=left)

    def kl_far(i):
        return item_copy(i, kl_s, kl_r, 2 * i + 1, i, seq=hop_l)

    def kl_has(i):
        return i <= z - half - 1

    def kl_sends(i):
        passes = (NS - 1 - z) % 2 == 0
        return passes & (i <= z - half - 3), passes & (i <= z - half - 2)

    def share_copy(lane, quarter, i, head):
        return Copy(kv.at[quarter, i], kv.at[quarter, i], kx_s.at[lane, i], kx_r.at[lane, i], head=head)

    def share(i):
        share_copy(1, mine_q, i, across).start()
        share_copy(0, mine_q, i, other).start()

    def relay(i):
        share_copy(1, across_q, i, across).came()
        share_copy(2, across_q, i, other).start()

    def gather(i):
        share_copy(0, twin_q, i, other).came()
        share_copy(2, last_q, i, other).came()

    def start_if(conditions, copies):
        for condition, copy in zip(conditions, copies):

            @pl.when(condition)
            def _(copy=copy):
                copy.start()

    start_if(kr_sends(0), (kr_far(0), kr_near(0)))
    direct = item_copy(z, kl_s, kl_r, 2 * early, z, seq=NS - 1)
    start_if((z < early,), (direct,))
    share(z)

    if paired:

        @pl.loop(1, NS)
        def _(d):
            for stream in range(2):
                ally_copy(stream, lax.rem(z + d, NS), 1 - turn).came()

    qrows = wq.shape[1] // (2 * HEAD_WIDTH)
    for i in range(qrows):
        at = 2 * i * HEAD_WIDTH
        q_att[i * rows : (i + 1) * rows, :] = (
            dot(normed[...], wq[:, at : at + HEAD_WIDTH]) * HEAD_WIDTH**-0.5
        ).astype(BF)
        g_att[i * rows : (i + 1) * rows, :] = dot(normed[...], wq[:, at + HEAD_WIDTH : at + 2 * HEAD_WIDTH])

    peak[...] = jnp.full(peak.shape, NEGATIVE, F32)
    total[...] = jnp.zeros(total.shape, F32)
    accum[...] = jnp.zeros(accum.shape, F32)

    def attend(items, own=False):
        parts = []
        for item in items:
            scores = dot_t(q_att[:, :PART], kv[0, item]) + dot_t(q_att[:, PART:], kv[1, item])
            n = qrows * rows if own else 1
            kpos = item * rows + lax.broadcasted_iota(jnp.int32, (n, rows), 1)
            visible = kpos < length
            if own:
                qpos = z * rows + lax.broadcasted_iota(jnp.int32, (n, rows), 0) % rows
                visible = visible & (kpos <= qpos)
            parts.append((item, jnp.where(visible, scores, NEGATIVE), visible))
        top = functools.reduce(jnp.maximum, [scores for _, scores, _ in parts])
        old = peak[...]
        new = jnp.maximum(old, jnp.max(top, -1, keepdims=True))
        scale = jnp.exp(old - new)
        peak[...] = new
        weights = [(item, jnp.where(visible, jnp.exp(scores - new), 0.0)) for item, scores, visible in parts]
        sums = functools.reduce(jnp.add, [w for _, w in weights])
        total[...] = total[...] * scale + jnp.sum(sums, -1, keepdims=True)
        weights = [(item, w.astype(BF)) for item, w in weights]
        for i in range(2):
            at = slice(i * PART, (i + 1) * PART)
            more = functools.reduce(jnp.add, [dot(w, kv[2 + i, item]) for item, w in weights])
            accum[:, at] = accum[:, at] * scale + more

    rounds = half // 2

    def items_of(k):
        near, far = z - (2 * k - 1), z - 2 * k
        turn_l = k - (NS - z) // 2
        i, j = 2 * turn_l - 2, 2 * turn_l - 1
        comes = turn_l >= 1
        return (near, near >= 0), (far, far >= 0), (i, comes & kl_has(i)), (j, comes & kl_has(j) & (j < early))

    def take(k):
        (near, has_near), (far, has_far), (i, has_i), (j, has_j) = items_of(k)
        for items, condition in (
            ((near, far, i, j), has_far & has_j),
            ((near, far), has_far & jnp.logical_not(has_j)),
            ((near,), has_near & jnp.logical_not(has_far)),
            ((i, j), has_j & jnp.logical_not(has_far)),
            ((i,), has_i & jnp.logical_not(has_j)),
        ):

            @pl.when(condition)
            def _(items=items):
                for item in items:
                    gather(item)
                attend(items)

    def pass_on(k):
        for item, condition in items_of(k):

            @pl.when(condition)
            def _(item=item):
                relay(item)

    @pl.loop(1, rounds + 3)
    def _(k):
        (near, has_near), (far, has_far), (i, has_i), (j, has_j) = items_of(k)

        @pl.when(has_far & (k <= rounds))
        def _():
            item_copy(far, kr_s, kr_r, 2 * k - 1, 2 * k - 1, seq=right).came()
            start_if(kr_sends(k), (kr_far(k), kr_near(k)))
            share(far)

        @pl.when(has_near & (k <= rounds))
        def _():
            item_copy(near, kr_s, kr_r, 2 * k - 2, 2 * k - 2, seq=right).came()
            share(near)

        for item, condition in ((i, has_i), (j, has_j)):

            @pl.when(condition & (k <= rounds))
            def _(item=item):
                item_copy(item, kl_s, kl_r, 2 * item, item, seq=left).came()
                start_if(kl_sends(item), (kl_far(item), kl_near(item)))
                share(item)

        @pl.when(k == 1)
        def _():
            relay(z)

        @pl.when((k > 1) & (k <= rounds + 1))
        def _():
            pass_on(k - 1)

        @pl.when(k == 2)
        def _():
            gather(z)
            attend((z,), own=True)

        @pl.when(k > 2)
        def _():
            take(k - 2)

    for i in range(qrows):
        at = slice(i * rows, (i + 1) * rows)
        o = accum[at, :] / total[at, 0:1] * sigmoid(g_att[at, :])
        attention_out[:, i * HEAD_WIDTH : (i + 1) * HEAD_WIDTH] = o.astype(BF)

    save.wait()
    halo_copy.sent()

    @pl.when(z == 0)
    def _():
        halo_copy.came()

    for d in range(2):
        for stream in range(2):
            for k in range(NS // 4):
                for c in weight_sends(stream, d, k):
                    c.sent()
    for c in stage + states + sums + gathers:
        c.sent()
    for s in range(1, ahead + 1):

        @pl.when(goes_right(s))
        def _(s=s):
            for k in range(CH):
                ag_right(s, k).sent()

    for s in range(1, wrapped + 1):

        @pl.when(goes_left(s))
        def _(s=s):
            for k in range(CH):
                ag_left(s, k).sent()


    def sent_if(conditions, copies):
        for condition, copy in zip(conditions, copies):

            @pl.when(condition)
            def _(copy=copy):
                copy.sent()

    sent_if((z < early,), (direct,))

    @pl.loop(0, rounds)
    def _(k):
        sent_if(kr_sends(k), (kr_far(k), kr_near(k)))

    @pl.loop(0, early)
    def _(i):
        sent_if(kl_sends(i), (kl_far(i), kl_near(i)))

    @pl.loop(0, z + 1)
    def _(i):
        for lane, quarter, to in ((0, mine_q, other), (1, mine_q, across), (2, across_q, other)):
            share_copy(lane, quarter, i, to).sent()

    if paired:

        @pl.loop(1, NS)
        def _(d):
            for stream in range(2):
                ally_copy(stream, lax.rem(z + d, NS)).sent()


def fine_right(a, b):
    bh, bl = halves(b)
    return dot(a, bh) + dot(a, bl)


def shards(NG, NS, NH, *args):
    (
        residual,
        query_in,
        key_in,
        value_in,
        gating_in,
        beta_logit,
        decay_logit,
        seq_length,
        conv_query,
        conv_key,
        conv_value,
        decay_rate,
        norm_gain,
        out_weight,
        attn_gain,
        query_weight,
        key_value_weight,
    ) = args
    rows, model = residual.shape
    kcols, vcols = query_in.shape[1], value_in.shape[1]
    heads = vcols // DV
    wcols = query_weight.shape[1]
    qheads = wcols // (2 * HEAD_WIDTH)
    nb = NS // heads
    half = NS // 2
    share = rows // NH
    ch = 4
    hbm = pl.BlockSpec(memory_space=pl.ANY)
    vmem = pl.BlockSpec(memory_space=pltpu.VMEM)
    smem = pl.BlockSpec(memory_space=pltpu.SMEM)
    dma = pltpu.SemaphoreType.DMA
    V = pltpu.VMEM
    scratch = [
        V((rows, 2 * kcols + vcols), BF),
        V((16, 2 * kcols + vcols), BF),
        V((rows + 8, 2 * kcols + vcols), F32),
        V((rows, vcols), BF),
        V((share, model), BF),
        V(out_weight.shape, BF),
        V((model, wcols), BF),
        V((model, PART), BF),
        V((heads, DK, DK + DV), BF),
        V((heads, DK, DK + DV), BF),
        V((DK, DK + DV), BF),
        V((nb // 2, DK, DK + DV), BF),
        V(((nb - 1) // 2, DK, DK + DV), BF),
        V((heads, DK, DK + DV), F32),
        V((DK, DK + DV), F32),
        V((DK, DV), F32),
        V((heads, DK, DV), BF),
        V((heads, DK, DV), BF),
        V((heads, rows, DK), F32),
        V((heads, rows, DV), F32),
        V((heads, rows, DK), F32),
        V((heads, rows, rows), F32),
        V((rows, vcols), BF),
        V((rows, model), F32),
        V((rows, model), BF),
        V((NH, share, model), BF),
        V((rows, model), BF),
        V((rows, model), BF),
        V((4, NS, rows, PART), BF),
        V((qheads * rows, HEAD_WIDTH), BF),
        V((qheads * rows, HEAD_WIDTH), F32),
        V((qheads * rows, 128), F32),
        V((qheads * rows, 128), F32),
        V((qheads * rows, HEAD_WIDTH), F32),
        dma((9,)),
        dma,
        dma,
        dma((2, 2, half)),
        dma((2, 2, half)),
        dma((2, half)),
        dma((2, half)),
        dma((2, NS)),
        dma((2, NS)),
        dma((heads,)),
        dma((heads,)),
        dma((2, nb // 2, ch)),
        dma((2, nb // 2, ch)),
        dma((heads,)),
        dma((heads,)),
        dma((NH,)),
        dma((NH,)),
        dma((NH,)),
        dma((NH,)),
        dma((half,)),
        dma((half,)),
        dma((2 * half,)),
        dma((half,)),
        dma((3, NS)),
        dma((3, NS)),
        *[pltpu.SemaphoreType.REGULAR] * 5,
    ]
    return pl.pallas_call(
        functools.partial(kernel, NG, NS, NH),
        name="layer",
        out_shape=(
            jax.ShapeDtypeStruct((rows, model), BF),
            jax.ShapeDtypeStruct((rows, qheads * HEAD_WIDTH), BF),
        ),
        in_specs=[hbm, hbm, hbm, hbm, hbm, vmem, vmem, smem, vmem, vmem, vmem, vmem, vmem, hbm, vmem, hbm, hbm],
        out_specs=(hbm, vmem),
        scratch_shapes=scratch,
        compiler_params=pltpu.CompilerParams(
            collective_id=0, has_side_effects=True, vmem_limit_bytes=56 * 1024 * 1024
        ),
    )(
        residual,
        query_in,
        key_in,
        value_in,
        gating_in,
        beta_logit.T,
        decay_logit.T,
        seq_length,
        conv_query,
        conv_key,
        conv_value,
        decay_rate.reshape(-1, 1),
        norm_gain.reshape(1, -1),
        out_weight,
        attn_gain.reshape(1, -1),
        query_weight,
        key_value_weight,
    )


def solution(mesh):
    placed = (
        P(("groups", "seq"), None),
        P(("groups", "seq"), "head"),
        P(("groups", "seq"), "head"),
        P(("groups", "seq"), "head"),
        P(("groups", "seq"), "head"),
        P(("groups", "seq"), "head"),
        P(("groups", "seq"), "head"),
        P("groups"),
        P(None, "head"),
        P(None, "head"),
        P(None, "head"),
        P("head"),
        P(),
        P("head", None),
        P(),
        P("seq", "head"),
        P("seq", None),
    )
    return jax.shard_map(
        functools.partial(shards, mesh.shape["groups"], mesh.shape["seq"], mesh.shape["head"]),
        mesh=mesh,
        in_specs=placed,
        out_specs=(P(("groups", "seq"), None), P(("groups", "seq"), "head")),
        check_vma=False,
    )
```

time: 247 us -> 152 us (0.62)
  the two profiles are of different devices: /device:TPU:4009 before, /device:TPU:2603 now
where the time goes in v2:
time: 152 us
  Pallas kernels  146 us (96%)
  local copies, waits for them, and re-layouts  4.76 us (3%)
    pallas_call x1, Pallas kernels, shards(): pl.pallas_call(functools.partial(kernel, NG, NS, NH), name='layer', out_s...  146 us
    unnamed x2, local copies, waits for them, and re-layouts  3.45 us

profile of v2, /device:TPU:2603, one launch (start us, length us, event | category | flops | bytes accessed | tf_op | source)
XLA Modules:
  0.0 152.0 jit_solution(5859176289912021978)
XLA Ops:
  1.3 1.3 copy.19.decay_rate
  2.6 146.0 %layer.1 = (bf16[128,2048]{1,0:T(8,128)(2,1)}, bf16[128,512]{1,0:T(8,128)(2,1)}) custom-call(bf16[128,2048]{1,0:T(8,128)(2,1)} %residual.1, bf16[128,256]{1,0:T(8,128)(2,1)} %query_in.1, bf16[128,256]{1,0:T(8,128)(2,1)} %key_in.1, bf16[128,512]{1,0:T(8,128)(2,1)} %value_in.1, bf16[128,512]{1,0:T(8,128)(2,1)} %gating_in.1, f32[4,128]{1,0:T(4,128)} %bitcast.6, ...), custom_call_target="tpu_custom_call" | custom-call | tf_op jit(solution)/shard_map/layer/pallas_call | solution.py:916
  148.6 1.9 %copy.23 = bf16[128,2048]{1,0:T(8,128)(2,1)} copy(bf16[128,2048]{1,0:T(8,128)(2,1)} %get-tuple-element.4) | data formatting | bytes 1048576
  150.4 1.6 %copy.24 = bf16[128,512]{1,0:T(8,128)(2,1)} copy(bf16[128,512]{1,0:T(8,128)(2,1)} %get-tuple-element.5) | data formatting | bytes 262144
